TPU v7x, 32 devices: a whole 2x2x4 slice. The times are simulated.
32 devices in a mesh: groups: 2 (over y), branch: 4 (over z), leaf: 4 (over x, core).
Axes of the slice: x: 2, y: 2, z: 4, core: 2. Of those that a mesh axis runs over, the one named last changes fastest.
Arguments:
- queries: float32 [4096, 1024], P(('groups', 'branch', 'leaf')), parts along dimension 0, may hold values from -32 to 32
- leaf_keys: float32 [4096, 128], P(('groups', 'branch', 'leaf')), parts along dimension 0, may hold values from -6 to 6
- leaf_values: float32 [4096, 128], P(('groups', 'branch', 'leaf')), parts along dimension 0, may hold values from -6 to 6
- root_keys: float32 [512, 128], P(('groups', 'branch', 'leaf')), parts along dimension 0, may hold values from -12 to 12
- root_values: float32 [512, 128], P(('groups', 'branch', 'leaf')), parts along dimension 0, may hold values from -6 to 6
- branch_keys: float32 [2048, 128], P(('groups', 'branch', 'leaf')), parts along dimension 0, may hold values from -6 to 6
- branch_values: float32 [2048, 128], P(('groups', 'branch', 'leaf')), parts along dimension 0, may hold values from -6 to 6
- d_out: float32 [4096, 1024], P(('groups', 'branch', 'leaf')), parts along dimension 0, may hold values from -6 to 6
- leaf_len: int32 [32], P(('groups', 'branch', 'leaf')), parts along dimension 0, may hold values from 1 to 128, 1280 in all
- leaf_parent: int32 [32], P(('groups', 'branch', 'leaf')), parts along dimension 0, may hold values from 0 to 255
- root_cut: int32 [8], P(('groups', 'branch')), parts along dimension 0, may hold values from 128 to 256
Outputs:
- attended: float32 [4096, 1024], P(('groups', 'branch', 'leaf')), parts along dimension 0
- d_queries: float32 [4096, 1024], P(('groups', 'branch', 'leaf')), parts along dimension 0
- d_root_kv: float32 [512, 256], P(('groups', 'branch', 'leaf')), parts along dimension 0
- d_branch_kv: float32 [2048, 256], P(('groups', 'branch', 'leaf')), parts along dimension 0
- d_leaf_kv: float32 [4096, 256], P(('groups', 'branch', 'leaf')), parts along dimension 0
There are 2 independent parts, one for each index of `groups`. A program takes and returns all parts, laid end to end along the dimension named above; each array names one. Nothing has to cross between parts.
Inputs may be any that keep to these rules, and one draw needn't show every extreme that they name: `leaf_len`: the lengths of one tree sum to 1280, and some leaf holds 128 live tokens.
All inputs are finite; a program needn't handle non-finite values. No bound on the sum of `leaf_len` on one device may be relied on, other than what follows from the above.
Results may differ from a plain program's by a relative error of at most 0.0003.
Values sent between devices are 32-bit elements; how exact they have to be, the bound alone decides.
A program may use at most 64 MiB of HBM per device.

v0:
```python
import functools
import math

import jax
import jax.numpy as jnp
from jax import lax
from jax.experimental import pallas as pl
from jax.experimental.pallas import tpu as pltpu
from jax.sharding import PartitionSpec as P

f32 = jnp.float32
bf16 = jnp.bfloat16
hidden = -1e30


def split2(x):
    high = x.astype(bf16)
    return high, (x - high.astype(f32)).astype(bf16)


def split3(x):
    high = x.astype(bf16)
    rest = x - high.astype(f32)
    middle = rest.astype(bf16)
    return high, middle, (rest - middle.astype(f32)).astype(bf16)


def mm(a, b):
    return lax.dot_general(a, b, (((1,), (0,)), ((), ())), preferred_element_type=f32)


def mmt(a, b):
    return lax.dot_general(a, b, (((1,), (1,)), ((), ())), preferred_element_type=f32)


def side(*parts):
    return jnp.concatenate(parts, axis=1)


def kernel(
    nb, nx, nc, dims,
    q_hbm, lk_hbm, lv_hbm, rk_hbm, rv_hbm, bk_hbm, bv_hbm, do_hbm, len_hbm, par_hbm, cut_hbm,
    att_ref, dqv_ref, droot_ref, dslice_ref, dleaf_ref,
    q_ref, do_ref, leaf_ref, rootb, sliceb,
    qs, cs, ks, vs, kt, vt, sc, dp, dkv,
    len_ref, par_ref, cut_ref,
    rc_root, rc_slice, sn_root, sn_slice, rv_root, rv_slice,
    ld_sem, gs_root, gr_root, gs_slice, gr_slice, cs_sem, cr_sem,
    ss_root, sr_root, ss_slice, sr_slice, es_sem, er_sem,
):
    T, H, D, r_rows, b_rows = dims
    R = T * H
    n_root = nb * nx * nc * r_rows
    n_slice = nx * nc * b_rows
    n_keys = n_root + n_slice + T
    scale = 1.0 / math.sqrt(D)
    g = lax.axis_index("groups")
    b = lax.axis_index("branch")
    leaf = lax.axis_index("leaf")
    x = leaf // nc
    c = leaf % nc
    pair = 2 * T if H % 2 == 0 else T
    per = pair // T
    n_pair = R // pair

    def dev(bb, xx, cc):
        return (g, bb, xx * nc + cc)

    def shifted(sb, sx):
        return lax.rem(b + sb, nb), lax.rem(x + sx, nx)

    peers = [(sb, sx) for sb in range(nb) for sx in range(nx) if sb or sx]
    other = lax.rem(c + 1, nc)

    loads = [
        (rk_hbm, rootb.at[b, x, c, 0]),
        (rv_hbm, rootb.at[b, x, c, 1]),
        (bk_hbm, sliceb.at[x, c, 0]),
        (bv_hbm, sliceb.at[x, c, 1]),
        (lk_hbm, leaf_ref.at[0]),
        (lv_hbm, leaf_ref.at[1]),
        (q_hbm, q_ref),
        (do_hbm, do_ref),
        (len_hbm, len_ref),
        (par_hbm, par_ref),
        (cut_hbm, cut_ref),
    ]
    loads = [pltpu.make_async_copy(s, d, ld_sem.at[i]) for i, (s, d) in enumerate(loads)]
    for cp in loads:
        cp.start()

    barrier = pltpu.get_barrier_semaphore()
    for sb, sx in peers:
        bb, xx = shifted(sb, sx)
        pl.semaphore_signal(barrier, inc=1, device_id=dev(bb, xx, c), device_id_type=pl.DeviceIdType.MESH)
    if nc == 2:
        pl.semaphore_signal(barrier, inc=1, device_id=dev(b, x, other), device_id_type=pl.DeviceIdType.MESH)
    pl.semaphore_wait(barrier, len(peers) + (nc == 2))

    def remote(src, dst, s_sem, r_sem, where):
        return pltpu.make_async_remote_copy(
            src_ref=src, dst_ref=dst, send_sem=s_sem, recv_sem=r_sem,
            device_id=where, device_id_type=pl.DeviceIdType.MESH,
        )

    for cp in loads[:4]:
        cp.wait()
    slice_sends, root_sends = [], []
    for sx in range(1, nx):
        bb, xx = shifted(0, sx)
        blk = sliceb.at[x, c]
        slice_sends.append(remote(blk, blk, gs_slice.at[sx], gr_slice.at[sx], dev(b, xx, c)))
    for i, (sb, sx) in enumerate(peers):
        bb, xx = shifted(sb, sx)
        blk = rootb.at[b, x, c]
        root_sends.append(remote(blk, blk, gs_root.at[i], gr_root.at[i], dev(bb, xx, c)))
    for cp in root_sends + slice_sends:
        cp.start()

    for cp in loads[4:]:
        cp.wait()
    live = lax.broadcasted_iota(jnp.int32, (T, D), 0) < len_ref[0]
    for h in range(H):
        cols = slice(h * D, (h + 1) * D)
        rows = slice(h * T, (h + 1) * T)
        q1, q2, q3 = split3(q_ref[:, cols])
        qs[0, rows], qs[1, rows], qs[2, rows] = q1, q2, q3
        c1, c2 = split2(jnp.where(live, do_ref[:, cols], 0.0))
        cs[0, rows], cs[1, rows] = c1, c2

    def stage(first, keys, values):
        count = keys.shape[0]
        span = slice(first, first + count)
        k1, k2, k3 = split3(keys)
        ks[span, :] = side(k1, k2, k3)
        v1, v2 = split2(values)
        vs[span, :] = side(v1, v2)
        ka, kb = split2(keys.T)
        kt[:D, span] = ka
        kt[D:, span] = kb
        va, vb = split2(values.T)
        vt[:D, span] = va
        vt[D:, span] = vb

    def score(first, count, seen):
        step = min(count, 256)

        def body(p, carry):
            rows = pl.ds(pl.multiple_of(p * pair, pair), pair)
            q1, q2, q3 = qs[0, rows, :], qs[1, rows, :], qs[2, rows, :]
            c1, c2 = cs[0, rows, :], cs[1, rows, :]
            qa, qb, qc = side(q1, q1), side(q2, q2), side(q3, q1)
            ca, cb = side(c1, c1), side(c2, c2)
            for lo in range(0, count, step):
                span = slice(first + lo, first + lo + step)
                k12 = ks[span, : 2 * D]
                k13 = side(ks[span, :D], ks[span, 2 * D :])
                s = mmt(k12, qa) + (mmt(k12, qb) + mmt(k13, qc))
                sc[span, rows] = jnp.where(seen(lo, step), s * scale, hidden)
                v12 = vs[span, :]
                dp[span, rows] = mmt(v12, ca) + mmt(v12, cb)
            return carry

        lax.fori_loop(0, n_pair, body, 0)

    def index_of(lo, step):
        return lo + lax.broadcasted_iota(jnp.int32, (step, pair), 0)

    def slot_of(step):
        return lax.broadcasted_iota(jnp.int32, (step, pair), 1) % T

    stage(n_root + n_slice, leaf_ref[0], leaf_ref[1])
    score(n_root + n_slice, T, lambda lo, step: index_of(lo, step) <= slot_of(step))

    core_sends = []
    for sx in range(1, nx):
        blk = sliceb.at[lax.rem(x + nx - sx, nx), c]
        remote(blk, blk, gs_slice.at[sx], gr_slice.at[sx], dev(b, x, c)).wait_recv()
    if nc == 2:
        cp = remote(sliceb.at[:, c], sliceb.at[:, c], cs_sem.at[0], cr_sem.at[0], dev(b, x, other))
        cp.start()
        core_sends.append(cp)
    for i, (sb, sx) in enumerate(peers):
        blk = rootb.at[lax.rem(b + nb - sb, nb), lax.rem(x + nx - sx, nx), c]
        remote(blk, blk, gs_root.at[i], gr_root.at[i], dev(b, x, c)).wait_recv()
    if nc == 2:
        cp = remote(rootb.at[:, :, c], rootb.at[:, :, c], cs_sem.at[1], cr_sem.at[1], dev(b, x, other))
        cp.start()
        core_sends.append(cp)
        remote(sliceb.at[:, other], sliceb.at[:, other], cs_sem.at[0], cr_sem.at[0], dev(b, x, other)).wait_recv()
    stage(
        n_root,
        sliceb[:, :, 0].reshape(n_slice, D),
        sliceb[:, :, 1].reshape(n_slice, D),
    )
    score(n_root, n_slice, lambda lo, step: index_of(lo, step) <= par_ref[0])
    if nc == 2:
        remote(rootb.at[:, :, other], rootb.at[:, :, other], cs_sem.at[1], cr_sem.at[1], dev(b, x, other)).wait_recv()
    stage(
        0,
        rootb[:, :, :, 0].reshape(n_root, D),
        rootb[:, :, :, 1].reshape(n_root, D),
    )
    score(0, n_root, lambda lo, step: index_of(lo, step) < cut_ref[0])

    chunk = 128

    def soften(p, carry):
        rows = pl.ds(pl.multiple_of(p * pair, pair), pair)
        spans = [slice(lo, lo + chunk) for lo in range(0, n_keys, chunk)]
        top = None
        for span in spans:
            m = jnp.max(sc[span, rows], axis=0, keepdims=True)
            top = m if top is None else jnp.maximum(top, m)
        total = jnp.zeros((1, pair), f32)
        dot = jnp.zeros((1, pair), f32)
        for span in spans:
            e = jnp.exp(sc[span, rows] - top)
            sc[span, rows] = e
            total = total + jnp.sum(e, axis=0, keepdims=True)
            dot = dot + jnp.sum(e * dp[span, rows], axis=0, keepdims=True)
        inverse = 1.0 / total
        dot = dot * inverse
        for span in spans:
            w = sc[span, rows] * inverse
            sc[span, rows] = w
            dp[span, rows] = w * (dp[span, rows] - dot) * scale
        return carry

    lax.fori_loop(0, n_pair, soften, 0)

    def key_gradients(first, step):
        span = pl.ds(first, step)
        s1, s2 = split2(dp[span, :])
        q12 = side(qs[0], qs[1])
        a = mm(s1, q12) + mm(s2, q12)
        w1, w2 = split2(sc[span, :])
        c12 = side(cs[0], cs[1])
        v = mm(w1, c12) + mm(w2, c12)
        return side(a[:, :D] + a[:, D:], v[:, :D] + v[:, D:])

    block = 2 * chunk if n_root % (2 * chunk) == 0 and n_slice % (2 * chunk) == 0 else chunk

    def gradient_block(i, carry):
        at = pl.multiple_of(i * block, block)
        dkv[pl.ds(at, block), :] = key_gradients(at, block)
        return carry

    root_g = dkv.at[:n_root].reshape(nb, nx, nc, r_rows, 2 * D)
    slice_g = dkv.at[n_root : n_root + n_slice].reshape(nx, nc, b_rows, 2 * D)
    lax.fori_loop(0, n_root // block, gradient_block, 0)
    ex = []
    if nc == 2:
        cp = remote(root_g.at[:, :, other], rc_root, es_sem.at[0], er_sem.at[0], dev(b, x, other))
        cp.start()
        ex.append(cp)
    lax.fori_loop(n_root // block, (n_root + n_slice) // block, gradient_block, 0)
    if nc == 2:
        cp = remote(slice_g.at[:, other], rc_slice, es_sem.at[1], er_sem.at[1], dev(b, x, other))
        cp.start()
        ex.append(cp)
        ex[0].wait_recv()
    mine = root_g[:, :, c]
    sn_root[...] = mine + rc_root[...] if nc == 2 else mine
    fin_root = []
    for i, (sb, sx) in enumerate(peers):
        bb, xx = shifted(sb, sx)
        fin_root.append(remote(sn_root.at[bb, xx], rv_root.at[i], ss_root.at[i], sr_root.at[i], dev(bb, xx, c)))
        fin_root[-1].start()
    if nc == 2:
        ex[1].wait_recv()
    mine = slice_g[:, c]
    sn_slice[...] = mine + rc_slice[...] if nc == 2 else mine
    fin_slice = []
    for sx in range(1, nx):
        bb, xx = shifted(0, sx)
        fin_slice.append(
            remote(sn_slice.at[xx], rv_slice.at[sx - 1], ss_slice.at[sx], sr_slice.at[sx], dev(b, xx, c))
        )
        fin_slice[-1].start()

    def outputs(p, carry):
        rows = pl.ds(pl.multiple_of(p * pair, pair), pair)
        w1, w2 = split2(sc[:, rows])
        m = mm(vt[...], w1) + mm(vt[...], w2)
        m = m[:D] + m[D:]
        s1, s2 = split2(dp[:, rows])
        n = mm(kt[...], s1) + mm(kt[...], s2)
        n = n[:D] + n[D:]
        for k in range(per):
            cols = pl.ds(pl.multiple_of(p * (per * D) + k * D, D), D)
            part = slice(k * T, (k + 1) * T)
            att_ref[:, cols] = jnp.where(live, m[:, part].T, 0.0)
            dqv_ref[:, cols] = n[:, part].T
        return carry

    lax.fori_loop(0, n_pair, outputs, 0)
    dleaf_ref[...] = key_gradients(n_root + n_slice, T)

    for cp in fin_slice:
        cp.wait_recv()
    total = sn_slice[x]
    for i in range(nx - 1):
        total = total + rv_slice[i]
    dslice_ref[...] = total
    for cp in fin_root:
        cp.wait_recv()
    total = sn_root[b, x]
    for i in range(len(peers)):
        total = total + rv_root[i]
    droot_ref[...] = total
    for cp in root_sends + slice_sends + core_sends + ex + fin_root + fin_slice:
        cp.wait_send()


def deliver(*refs):
    sources, targets, sem = refs[:5], refs[5:10], refs[10]
    copies = [pltpu.make_async_copy(s, t, sem.at[i]) for i, (s, t) in enumerate(zip(sources, targets))]
    for cp in copies:
        cp.start()
    for cp in copies:
        cp.wait()


def shards(mesh, *args):
    queries, leaf_keys, _, root_keys, _, branch_keys = args[:6]
    T, width = queries.shape
    D = leaf_keys.shape[1]
    H = width // D
    r_rows, b_rows = root_keys.shape[0], branch_keys.shape[0]
    nb, nl = mesh.shape["branch"], mesh.shape["leaf"]
    nc = 2 if nl % 2 == 0 else 1
    nx = nl // nc
    R = T * H
    n_root, n_slice = nb * nl * r_rows, nl * b_rows
    n_keys = n_root + n_slice + T
    any_space = pl.BlockSpec(memory_space=pl.ANY)
    hbm = pl.BlockSpec(memory_space=pltpu.HBM)
    vmem = pl.BlockSpec(memory_space=pltpu.VMEM)
    V = pltpu.VMEM
    S = pltpu.SMEM
    dma = pltpu.SemaphoreType.DMA
    np_ = max(nb * nx - 1, 1)
    scratch = [
        V((T, width), f32), V((T, width), f32), V((2, T, D), f32),
        V((nb, nx, nc, 2, r_rows, D), f32), V((nx, nc, 2, b_rows, D), f32),
        V((3, R, D), bf16), V((2, R, D), bf16),
        V((n_keys, 3 * D), bf16), V((n_keys, 2 * D), bf16),
        V((2 * D, n_keys), bf16), V((2 * D, n_keys), bf16),
        V((n_keys, R), f32), V((n_keys, R), f32), V((n_root + n_slice, 2 * D), f32),
        S((1,), jnp.int32), S((1,), jnp.int32), S((1,), jnp.int32),
        V((nb, nx, r_rows, 2 * D), f32), V((nx, b_rows, 2 * D), f32),
        V((nb, nx, r_rows, 2 * D), f32), V((nx, b_rows, 2 * D), f32),
        V((np_, r_rows, 2 * D), f32), V((max(nx - 1, 1), b_rows, 2 * D), f32),
        dma((11,)), dma((np_,)), dma((np_,)), dma((nx,)), dma((nx,)), dma((2,)), dma((2,)),
        dma((np_,)), dma((np_,)), dma((nx,)), dma((nx,)), dma((2,)), dma((2,)),
    ]
    shape = lambda *s: V(s, f32)
    sizes = ((T, width), (T, width), (r_rows, 2 * D), (b_rows, 2 * D), (T, 2 * D))
    held = pl.pallas_call(
        functools.partial(kernel, nb, nx, nc, (T, H, D, r_rows, b_rows)),
        out_shape=tuple(shape(*size) for size in sizes),
        in_specs=[any_space] * 8 + [hbm] * 3,
        out_specs=(vmem,) * 5,
        scratch_shapes=scratch,
        compiler_params=pltpu.CompilerParams(
            collective_id=0, has_side_effects=True, vmem_limit_bytes=60 * 1024 * 1024
        ),
        name="tree",
    )(*args)
    return pl.pallas_call(
        deliver,
        out_shape=tuple(jax.ShapeDtypeStruct(size, f32) for size in sizes),
        in_specs=[vmem] * 5,
        out_specs=(any_space,) * 5,
        scratch_shapes=[dma((5,))],
        compiler_params=pltpu.CompilerParams(vmem_limit_bytes=1024 * 1024),
        name="deliver",
    )(*held)


def solution(mesh):
    rows = P(("groups", "branch", "leaf"), None)
    flat = P(("groups", "branch", "leaf"))
    return jax.shard_map(
        functools.partial(shards, mesh),
        mesh=mesh,
        in_specs=(rows,) * 8 + (flat, flat, P(("groups", "branch"))),
        out_specs=(rows,) * 5,
        check_vma=False,
    )
```

profile of v0, /device:TPU:0, one launch (start us, length us, event | category | flops | bytes accessed | tf_op | source)
XLA Modules:
  0.0 27.2 jit_solution(4323116606627559640)
XLA Ops:
  2.6 23.5 %tree.1 = (f32[128,1024]{1,0:T(8,128)S(1)}, f32[128,1024]{1,0:T(8,128)S(1)}, f32[16,256]{1,0:T(8,128)S(1)}, f32[64,256]{1,0:T(8,128)S(1)}, f32[128,256]{1,0:T(8,128)S(1)}) custom-call(f32[128,1024]{1,0:T(8,128)} %q_hbm.1, f32[128,128]{1,0:T(8,128)} %lk_hbm.1, f32[128,128]{1,0:T(8,128)} %lv_hbm.1, f32[16,128]{1,0:T(8,128)} %rk_hbm.1, f32[16,128]{1,0:T(8,128)} %rv_hbm.1, ...), custom_call_target="tpu_custom_call" | custom-call | tf_op jit(solution)/shard_map/tree/pallas_call | solution.py:360
  26.1 1.1 %deliver.1 = (f32[128,1024]{1,0:T(8,128)}, f32[128,1024]{1,0:T(8,128)}, f32[16,256]{1,0:T(8,128)}, f32[64,256]{1,0:T(8,128)}, f32[128,256]{1,0:T(8,128)}) custom-call(f32[128,1024]{1,0:T(8,128)S(1)} %get-tuple-element.10.refs_0_, f32[128,1024]{1,0:T(8,128)S(1)} %get-tuple-element.11.refs_1_, f32[16,256]{1,0:T(8,128)S(1)} %get-tuple-element.12.refs_2_, ...), custom_call_target="tpu_custom_call" | custom-call | tf_op jit(solution)/shard_map/deliver/pallas_call | solution.py:371
where the time goes:
time: 27.3 us; the launch traced here: 27.2 us
  Pallas kernels  24.6 us (90%)
  between operations  2.58 us (9%)
    pallas_call x1, Pallas kernels, shards(): pl.pallas_call(functools.partial(kernel, nb, nx, nc, (T, H, D, r_rows, b_...  23.5 us
    pallas_call x1, Pallas kernels, shards(): pl.pallas_call(deliver, out_shape=tuple((jax.ShapeDtypeStruct(size, f32)...  1.07 us

commit v1 on v0

v1 whole, which is shorter than its diff:
```python
import functools
import math

import jax
import jax.numpy as jnp
from jax import lax
from jax.experimental import pallas as pl
from jax.experimental.pallas import tpu as pltpu
from jax.sharding import PartitionSpec as P

f32 = jnp.float32
bf16 = jnp.bfloat16
hidden = -1e30


def split2(x):
    high = x.astype(bf16)
    return high, (x - high.astype(f32)).astype(bf16)


def split3(x):
    high = x.astype(bf16)
    rest = x - high.astype(f32)
    middle = rest.astype(bf16)
    return high, middle, (rest - middle.astype(f32)).astype(bf16)


def mm(a, b):
    return lax.dot_general(a, b, (((1,), (0,)), ((), ())), preferred_element_type=f32)


def mmt(a, b):
    return lax.dot_general(a, b, (((1,), (1,)), ((), ())), preferred_element_type=f32)


def side(*parts):
    return jnp.concatenate(parts, axis=1)


def kernel(
    nb, nx, nc, dims,
    q_hbm, lk_hbm, lv_hbm, rk_hbm, rv_hbm, bk_hbm, bv_hbm, do_hbm, len_hbm, par_hbm, cut_hbm,
    att_ref, dqv_ref, droot_ref, dslice_ref, dleaf_ref,
    qd_ref, leaf_ref, rootb, sliceb,
    qs, cs, qt, ct, ks, vs, kt, vt, sc, dp, dkv, top_c, sum_c, dot_c, fac_c, dot_r,
    len_ref, par_ref, cut_ref,
    rc_root, rc_slice, sn_root, sn_slice, rv_root, rv_slice,
    ld_sem, gs_root, gr_root, gs_slice, gr_slice, cs_sem, cr_sem,
    ss_root, sr_root, ss_slice, sr_slice, es_sem, er_sem,
):
    T, H, D, r_rows, b_rows = dims
    R = T * H
    n_root = nb * nx * nc * r_rows
    n_part = nc * b_rows
    n_slice = nx * n_part
    n_keys = n_root + n_slice + T
    scale = 1.0 / math.sqrt(D)
    g = lax.axis_index("groups")
    b = lax.axis_index("branch")
    leaf = lax.axis_index("leaf")
    x = leaf // nc
    c = leaf % nc
    pair = 2 * T if H % 2 == 0 else T
    per = pair // T
    n_pair = R // pair

    def dev(bb, xx, cc):
        return (g, bb, xx * nc + cc)

    def shifted(sb, sx):
        return lax.rem(b + sb, nb), lax.rem(x + sx, nx)

    peers = [(sb, sx) for sb in range(nb) for sx in range(nx) if sb or sx]
    other = lax.rem(c + 1, nc)

    loads = [
        [(rk_hbm, rootb.at[b, x, c, 0]), (rv_hbm, rootb.at[b, x, c, 1])],
        [(bk_hbm, sliceb.at[x, c, 0]), (bv_hbm, sliceb.at[x, c, 1])],
        [(q_hbm, qd_ref.at[0]), (do_hbm, qd_ref.at[1])],
        [(lk_hbm, leaf_ref.at[0]), (lv_hbm, leaf_ref.at[1])],
        [(len_hbm, len_ref)],
        [(par_hbm, par_ref)],
        [(cut_hbm, cut_ref)],
    ]
    for i, group in enumerate(loads):
        for source, target in group:
            pltpu.make_async_copy(source, target, ld_sem.at[i]).start()

    def loaded(i, target):
        pltpu.make_async_copy(target, target, ld_sem.at[i]).wait()

    barrier = pltpu.get_barrier_semaphore()
    for sb, sx in peers:
        bb, xx = shifted(sb, sx)
        pl.semaphore_signal(barrier, inc=1, device_id=dev(bb, xx, c), device_id_type=pl.DeviceIdType.MESH)
    if nc == 2:
        pl.semaphore_signal(barrier, inc=1, device_id=dev(b, x, other), device_id_type=pl.DeviceIdType.MESH)
    loaded(0, rootb.at[b, x, c])
    loaded(1, sliceb.at[x, c])
    pl.semaphore_wait(barrier, len(peers) + (nc == 2))

    def remote(src, dst, s_sem, r_sem, where):
        return pltpu.make_async_remote_copy(
            src_ref=src, dst_ref=dst, send_sem=s_sem, recv_sem=r_sem,
            device_id=where, device_id_type=pl.DeviceIdType.MESH,
        )

    own = rootb.at[b, x, c]
    for sb, sx in peers:
        bb, xx = shifted(sb, sx)
        remote(own, own, gs_root, gr_root, dev(bb, xx, c)).start()
    own = sliceb.at[x, c]
    for sx in range(1, nx):
        bb, xx = shifted(0, sx)
        remote(own, own, gs_slice, gr_slice.at[sx], dev(b, xx, c)).start()
    core_sends = []

    def to_sibling(ref, i):
        core_sends.append(remote(ref, ref, cs_sem.at[i], cr_sem.at[i], dev(b, x, other)))
        core_sends[-1].start()

    def from_sibling(ref, i):
        remote(ref, ref, cs_sem.at[i], cr_sem.at[i], dev(b, x, other)).wait_recv()

    if nc == 2:
        to_sibling(own, 0)

    loaded(2, qd_ref)
    loaded(3, leaf_ref)
    loaded(4, len_ref)
    loaded(5, par_ref)
    loaded(6, cut_ref)
    live = lax.broadcasted_iota(jnp.int32, (T, D), 0) < len_ref[0]
    for h in range(H):
        cols = slice(h * D, (h + 1) * D)
        rows = slice(h * T, (h + 1) * T)
        q = qd_ref[0, :, cols]
        q1, q2 = split2(q)
        qs[rows, :] = side(q1, q2)
        q1, q2, q3 = split3(q.T)
        qt[0, :D, rows], qt[0, D:, rows] = q1, q1
        qt[1, :D, rows], qt[1, D:, rows] = q2, q2
        qt[2, :D, rows], qt[2, D:, rows] = q3, q1
        d = jnp.where(live, qd_ref[1, :, cols], 0.0)
        c1, c2 = split2(d)
        cs[rows, :] = side(c1, c2)
        c1, c2 = split2(d.T)
        ct[0, :D, rows], ct[0, D:, rows] = c1, c1
        ct[1, :D, rows], ct[1, D:, rows] = c2, c2

    def stage(first, keys, values):
        span = slice(first, first + keys.shape[0])
        k1, k2, k3 = split3(keys)
        ks[span, :] = side(k1, k2, k1, k3)
        v1, v2 = split2(values)
        vs[span, :] = side(v1, v2)

    def stage_across(first, keys, values):
        span = slice(first, first + keys.shape[0])
        ka, kb = split2(keys.T)
        kt[:D, span] = ka
        kt[D:, span] = kb
        va, vb = split2(values.T)
        vt[:D, span] = va
        vt[D:, span] = vb

    def score(chunk, first, count, seen, wide):
        span = slice(first, first + count)
        k12, k13, v12 = ks.at[span, : 2 * D], ks.at[span, 2 * D :], vs.at[span, :]

        def body(p):
            rows = pl.ds(pl.multiple_of(p * pair, pair), pair)
            s = mm(k12[...], qt[0, :, rows]) + (mm(k12[...], qt[1, :, rows]) + mm(k13[...], qt[2, :, rows]))
            s = jnp.where(seen(count), s * scale, hidden)
            m = jnp.max(s, axis=0, keepdims=True)
            g = mm(v12[...], ct[0, :, rows]) + mm(v12[...], ct[1, :, rows])
            e = jnp.exp(s - m)
            sc[span, rows] = e
            dp[span, rows] = g
            top_c[chunk : chunk + 1, rows] = m
            sum_c[chunk : chunk + 1, rows] = jnp.sum(e, axis=0, keepdims=True)
            dot_c[chunk : chunk + 1, rows] = jnp.sum(e * g, axis=0, keepdims=True)

        def trip(i, carry):
            for k in range(wide):
                body(i * wide + k)
            return carry

        if n_pair == wide:
            trip(0, 0)
        else:
            lax.fori_loop(0, n_pair // wide, trip, 0)

    def index_of(step):
        return lax.broadcasted_iota(jnp.int32, (step, pair), 0)

    def slot_of(step):
        return lax.broadcasted_iota(jnp.int32, (step, pair), 1) % T

    step = 256 if n_root % 256 == 0 else 128
    at_leaf = n_root + n_slice
    chunks = [(at_leaf, T)]
    chunks += [(n_root + sx * n_part, n_part) for sx in range(nx)]
    chunks += [(lo, step) for lo in range(0, n_root, step)]
    two = 2 if n_pair % 2 == 0 else 1

    stage(at_leaf, leaf_ref[0], leaf_ref[1])
    score(0, at_leaf, T, lambda step: index_of(step) <= slot_of(step), two)

    def score_part(sx):
        bb, xx = shifted(0, sx)
        first, count = chunks[1 + sx]
        stage(first, sliceb[xx, :, 0].reshape(count, D), sliceb[xx, :, 1].reshape(count, D))
        score(1 + sx, first, count, lambda step: xx * n_part + index_of(step) <= par_ref[0], two)

    if nc == 2:
        from_sibling(sliceb.at[x, other], 0)
    score_part(0)

    for sx in range(1, nx):
        bb, xx = shifted(0, nx - sx)
        blk = sliceb.at[xx, c]
        remote(blk, blk, gs_slice, gr_slice.at[sx], dev(b, x, c)).wait_recv()
        if nc == 2:
            to_sibling(blk, 1 + nx - sx)
    remote(rv_root, rv_root, gs_root, gr_root, dev(b, x, c)).wait_recv()
    if nc == 2:
        to_sibling(rootb.at[:, :, c], 1)
    for sx in range(1, nx):
        bb, xx = shifted(0, sx)
        if nc == 2:
            from_sibling(sliceb.at[xx, other], 1 + sx)
        score_part(sx)
    if nc == 2:
        from_sibling(rootb.at[:, :, other], 1)
    stage(0, rootb[:, :, :, 0].reshape(n_root, D), rootb[:, :, :, 1].reshape(n_root, D))
    for i, (first, count) in enumerate(chunks[1 + nx :]):
        score(
            1 + nx + i, first, count, lambda step: first + index_of(step) < cut_ref[0],
            n_pair if n_root == step else two,
        )

    tops = top_c[...]
    factor = jnp.exp(tops - jnp.max(tops, axis=0, keepdims=True))
    inverse = 1.0 / jnp.sum(factor * sum_c[...], axis=0, keepdims=True)
    fac_c[...] = factor * inverse
    dot_r[...] = jnp.sum(factor * dot_c[...], axis=0, keepdims=True) * inverse

    def weights(chunk, rows):
        first, count = chunks[chunk]
        span = slice(first, first + count)
        w = sc[span, rows] * fac_c[chunk : chunk + 1, rows]
        return split2(w), split2(w * ((dp[span, rows] - dot_r[:, rows]) * scale))

    def key_gradients(chunk):
        (w1, w2), (s1, s2) = weights(chunk, slice(None))
        a = mm(s1, qs[...]) + mm(s2, qs[...])
        v = mm(w1, cs[...]) + mm(w2, cs[...])
        return side(a[:, :D] + a[:, D:], v[:, :D] + v[:, D:])

    def block_gradients(chunk):
        first, count = chunks[chunk]
        dkv[first : first + count, :] = key_gradients(chunk)

    root_g = dkv.at[:n_root].reshape(nb, nx, nc, r_rows, 2 * D)
    slice_g = dkv.at[n_root : n_root + n_slice].reshape(nx, nc, b_rows, 2 * D)
    for i in range(1 + nx, len(chunks)):
        block_gradients(i)
    ex = []
    if nc == 2:
        ex.append(remote(root_g.at[:, :, other], rc_root, es_sem.at[0], er_sem.at[0], dev(b, x, other)))
        ex[0].start()
    for sx in range(nx):
        block_gradients(1 + sx)
    if nc == 2:
        ex.append(remote(slice_g.at[:, other], rc_slice, es_sem.at[1], er_sem.at[1], dev(b, x, other)))
        ex[1].start()
        ex[0].wait_recv()
    mine = root_g[:, :, c]
    sn_root[...] = mine + rc_root[...] if nc == 2 else mine
    for i, (sb, sx) in enumerate(peers):
        bb, xx = shifted(sb, sx)
        remote(sn_root.at[bb, xx], rv_root.at[i], ss_root, sr_root, dev(bb, xx, c)).start()

    stage_across(0, rootb[:, :, :, 0].reshape(n_root, D), rootb[:, :, :, 1].reshape(n_root, D))
    for sx in range(nx):
        bb, xx = shifted(0, sx)
        first, count = chunks[1 + sx]
        stage_across(first, sliceb[xx, :, 0].reshape(count, D), sliceb[xx, :, 1].reshape(count, D))
    stage_across(at_leaf, leaf_ref[0], leaf_ref[1])

    if nc == 2:
        ex[1].wait_recv()
    mine = slice_g[:, c]
    sn_slice[...] = mine + rc_slice[...] if nc == 2 else mine
    for sx in range(1, nx):
        bb, xx = shifted(0, sx)
        remote(sn_slice.at[sx], rv_slice.at[sx - 1], ss_slice, sr_slice, dev(b, xx, c)).start()

    def outputs(p, carry):
        rows = pl.ds(pl.multiple_of(p * pair, pair), pair)
        m, n = None, None
        for chunk, (first, count) in enumerate(chunks):
            span = slice(first, first + count)
            (w1, w2), (s1, s2) = weights(chunk, rows)
            part = mm(vt[:, span], w1) + mm(vt[:, span], w2)
            m = part if m is None else m + part
            part = mm(kt[:, span], s1) + mm(kt[:, span], s2)
            n = part if n is None else n + part
        m = m[:D] + m[D:]
        n = n[:D] + n[D:]
        for k in range(per):
            cols = pl.ds(pl.multiple_of(p * (per * D) + k * D, D), D)
            part = slice(k * T, (k + 1) * T)
            att_ref[:, cols] = jnp.where(live, m[:, part].T, 0.0)
            dqv_ref[:, cols] = n[:, part].T
        return carry

    lax.fori_loop(0, n_pair, outputs, 0)
    dleaf_ref[...] = key_gradients(0)

    total = sn_slice[0]
    if nx > 1:
        remote(rv_slice, rv_slice, ss_slice, sr_slice, dev(b, x, c)).wait_recv()
        for i in range(nx - 1):
            total = total + rv_slice[i]
    dslice_ref[...] = total
    total = sn_root[b, x]
    if peers:
        remote(rv_root, rv_root, ss_root, sr_root, dev(b, x, c)).wait_recv()
        for i in range(len(peers)):
            total = total + rv_root[i]
    droot_ref[...] = total
    for cp in core_sends + ex:
        cp.wait_send()
    if peers:
        remote(rv_root, rv_root, gs_root, gr_root, dev(b, x, c)).wait_send()
        remote(rv_root, rv_root, ss_root, sr_root, dev(b, x, c)).wait_send()
    if nx > 1:
        remote(rv_slice, rv_slice, gs_slice, gr_slice.at[0], dev(b, x, c)).wait_send()
        remote(rv_slice, rv_slice, ss_slice, sr_slice, dev(b, x, c)).wait_send()


def deliver(*refs):
    sources, targets, sem = refs[:5], refs[5:10], refs[10]
    copies = [pltpu.make_async_copy(s, t, sem.at[i]) for i, (s, t) in enumerate(zip(sources, targets))]
    for cp in copies:
        cp.start()
    for cp in copies:
        cp.wait()


def shards(mesh, *args):
    queries, leaf_keys, _, root_keys, _, branch_keys = args[:6]
    T, width = queries.shape
    D = leaf_keys.shape[1]
    H = width // D
    r_rows, b_rows = root_keys.shape[0], branch_keys.shape[0]
    nb, nl = mesh.shape["branch"], mesh.shape["leaf"]
    nc = 2 if nl % 2 == 0 else 1
    nx = nl // nc
    R = T * H
    n_root, n_slice = nb * nl * r_rows, nl * b_rows
    n_keys = n_root + n_slice + T
    n_chunks = 1 + nx + n_root // (256 if n_root % 256 == 0 else 128)
    any_space = pl.BlockSpec(memory_space=pl.ANY)
    hbm = pl.BlockSpec(memory_space=pltpu.HBM)
    vmem = pl.BlockSpec(memory_space=pltpu.VMEM)
    V = pltpu.VMEM
    S = pltpu.SMEM
    dma = pltpu.SemaphoreType.DMA
    np_ = max(nb * nx - 1, 1)
    scratch = [
        V((2, T, width), f32), V((2, T, D), f32),
        V((nb, nx, nc, 2, r_rows, D), f32), V((nx, nc, 2, b_rows, D), f32),
        V((R, 2 * D), bf16), V((R, 2 * D), bf16), V((3, 2 * D, R), bf16), V((2, 2 * D, R), bf16),
        V((n_keys, 4 * D), bf16), V((n_keys, 2 * D), bf16),
        V((2 * D, n_keys), bf16), V((2 * D, n_keys), bf16),
        V((n_keys, R), f32), V((n_keys, R), f32), V((n_root + n_slice, 2 * D), f32),
        V((n_chunks, R), f32), V((n_chunks, R), f32), V((n_chunks, R), f32), V((n_chunks, R), f32), V((1, R), f32),
        S((1,), jnp.int32), S((1,), jnp.int32), S((1,), jnp.int32),
        V((nb, nx, r_rows, 2 * D), f32), V((nx, b_rows, 2 * D), f32),
        V((nb, nx, r_rows, 2 * D), f32), V((nx, b_rows, 2 * D), f32),
        V((np_, r_rows, 2 * D), f32), V((max(nx - 1, 1), b_rows, 2 * D), f32),
        dma((7,)), dma, dma, dma, dma((nx,)), dma((1 + nx,)), dma((1 + nx,)),
        dma, dma, dma, dma, dma((2,)), dma((2,)),
    ]
    shape = lambda *s: V(s, f32)
    sizes = ((T, width), (T, width), (r_rows, 2 * D), (b_rows, 2 * D), (T, 2 * D))
    held = pl.pallas_call(
        functools.partial(kernel, nb, nx, nc, (T, H, D, r_rows, b_rows)),
        out_shape=tuple(shape(*size) for size in sizes),
        in_specs=[any_space] * 8 + [hbm] * 3,
        out_specs=(vmem,) * 5,
        scratch_shapes=scratch,
        compiler_params=pltpu.CompilerParams(
            collective_id=0, has_side_effects=True, vmem_limit_bytes=60 * 1024 * 1024
        ),
        name="tree",
    )(*args)
    return pl.pallas_call(
        deliver,
        out_shape=tuple(jax.ShapeDtypeStruct(size, f32) for size in sizes),
        in_specs=[vmem] * 5,
        out_specs=(any_space,) * 5,
        scratch_shapes=[dma((5,))],
        compiler_params=pltpu.CompilerParams(vmem_limit_bytes=1024 * 1024),
        name="deliver",
    )(*held)


def solution(mesh):
    rows = P(("groups", "branch", "leaf"), None)
    flat = P(("groups", "branch", "leaf"))
    return jax.shard_map(
        functools.partial(shards, mesh),
        mesh=mesh,
        in_specs=(rows,) * 8 + (flat, flat, P(("groups", "branch"))),
        out_specs=(rows,) * 5,
        check_vma=False,
    )
```

time: 27.3 us -> 24 us (0.88)
  Pallas kernels: 24.6 us -> 21.2 us
    pallas_call x1, Pallas kernels: 23.5 us -> 20.1 us  [shards(): pl.pallas_call(functools.partial(kernel, nb, nx, nc, (T, H, D, r_rows, b_...]
where the time goes in v1:
time: 24 us; the launch traced here: 23.8 us
  Pallas kernels  21.2 us (88%)
  between operations  2.58 us (11%)
    pallas_call x1, Pallas kernels, shards(): pl.pallas_call(functools.partial(kernel, nb, nx, nc, (T, H, D, r_rows, b_...  20.1 us
    pallas_call x1, Pallas kernels, shards(): pl.pallas_call(deliver, out_shape=tuple((jax.ShapeDtypeStruct(size, f32)...  1.07 us

profile of v1, /device:TPU:0, one launch (start us, length us, event | category | flops | bytes accessed | tf_op | source)
XLA Modules:
  0.0 23.8 jit_solution(908667608247342251)
XLA Ops:
  2.6 20.1 %tree.1 = (f32[128,1024]{1,0:T(8,128)S(1)}, f32[128,1024]{1,0:T(8,128)S(1)}, f32[16,256]{1,0:T(8,128)S(1)}, f32[64,256]{1,0:T(8,128)S(1)}, f32[128,256]{1,0:T(8,128)S(1)}) custom-call(f32[128,1024]{1,0:T(8,128)} %q_hbm.1, f32[128,128]{1,0:T(8,128)} %lk_hbm.1, f32[128,128]{1,0:T(8,128)} %lv_hbm.1, f32[16,128]{1,0:T(8,128)} %rk_hbm.1, f32[16,128]{1,0:T(8,128)} %rv_hbm.1, ...), custom_call_target="tpu_custom_call" | custom-call | tf_op jit(solution)/shard_map/tree/pallas_call | solution.py:390
  22.7 1.1 %deliver.1 = (f32[128,1024]{1,0:T(8,128)}, f32[128,1024]{1,0:T(8,128)}, f32[16,256]{1,0:T(8,128)}, f32[64,256]{1,0:T(8,128)}, f32[128,256]{1,0:T(8,128)}) custom-call(f32[128,1024]{1,0:T(8,128)S(1)} %get-tuple-element.10.refs_0_, f32[128,1024]{1,0:T(8,128)S(1)} %get-tuple-element.11.refs_1_, f32[16,256]{1,0:T(8,128)S(1)} %get-tuple-element.12.refs_2_, ...), custom_call_target="tpu_custom_call" | custom-call | tf_op jit(solution)/shard_map/deliver/pallas_call | solution.py:401

commit v2 on v1

--- a/solution.py
+++ b/solution.py
@@ -71,6 +71,7 @@
         return lax.rem(b + sb, nb), lax.rem(x + sx, nx)
 
     peers = [(sb, sx) for sb in range(nb) for sx in range(nx) if sb or sx]
+    peers.sort(key=lambda p: (p[1] == 0, -min(p[0], nb - p[0])))
     other = lax.rem(c + 1, nc)
 
     loads = [

time: 24 us -> 23.7 us (0.987)
  Pallas kernels: 21.2 us -> 20.9 us
    pallas_call x1, Pallas kernels: 20.1 us -> 19.8 us  [shards(): pl.pallas_call(functools.partial(kernel, nb, nx, nc, (T, H, D, r_rows, b_...]
where the time goes in v2:
time: 23.7 us; the launch traced here: 23.5 us
  Pallas kernels  20.9 us (88%)
  between operations  2.58 us (11%)
    pallas_call x1, Pallas kernels, shards(): pl.pallas_call(functools.partial(kernel, nb, nx, nc, (T, H, D, r_rows, b_...  19.8 us
    pallas_call x1, Pallas kernels, shards(): pl.pallas_call(deliver, out_shape=tuple((jax.ShapeDtypeStruct(size, f32)...  1.07 us

profile of v2, /device:TPU:0, one launch (start us, length us, event | category | flops | bytes accessed | tf_op | source)
XLA Modules:
  0.0 23.5 jit_solution(1407933983692995120)
XLA Ops:
  2.6 19.8 %tree.1 = (f32[128,1024]{1,0:T(8,128)S(1)}, f32[128,1024]{1,0:T(8,128)S(1)}, f32[16,256]{1,0:T(8,128)S(1)}, f32[64,256]{1,0:T(8,128)S(1)}, f32[128,256]{1,0:T(8,128)S(1)}) custom-call(f32[128,1024]{1,0:T(8,128)} %q_hbm.1, f32[128,128]{1,0:T(8,128)} %lk_hbm.1, f32[128,128]{1,0:T(8,128)} %lv_hbm.1, f32[16,128]{1,0:T(8,128)} %rk_hbm.1, f32[16,128]{1,0:T(8,128)} %rv_hbm.1, ...), custom_call_target="tpu_custom_call" | custom-call | tf_op jit(solution)/shard_map/tree/pallas_call | solution.py:391
  22.4 1.1 %deliver.1 = (f32[128,1024]{1,0:T(8,128)}, f32[128,1024]{1,0:T(8,128)}, f32[16,256]{1,0:T(8,128)}, f32[64,256]{1,0:T(8,128)}, f32[128,256]{1,0:T(8,128)}) custom-call(f32[128,1024]{1,0:T(8,128)S(1)} %get-tuple-element.10.refs_0_, f32[128,1024]{1,0:T(8,128)S(1)} %get-tuple-element.11.refs_1_, f32[16,256]{1,0:T(8,128)S(1)} %get-tuple-element.12.refs_2_, ...), custom_call_target="tpu_custom_call" | custom-call | tf_op jit(solution)/shard_map/deliver/pallas_call | solution.py:402

commit v3 on v2

--- a/solution.py
+++ b/solution.py
@@ -72,6 +72,7 @@
 
     peers = [(sb, sx) for sb in range(nb) for sx in range(nx) if sb or sx]
     peers.sort(key=lambda p: (p[1] == 0, -min(p[0], nb - p[0])))
+    columns = list(range(1, nx)) + [0]
     other = lax.rem(c + 1, nc)
 
     loads = [
@@ -97,7 +98,6 @@
     if nc == 2:
         pl.semaphore_signal(barrier, inc=1, device_id=dev(b, x, other), device_id_type=pl.DeviceIdType.MESH)
     loaded(0, rootb.at[b, x, c])
-    loaded(1, sliceb.at[x, c])
     pl.semaphore_wait(barrier, len(peers) + (nc == 2))
 
     def remote(src, dst, s_sem, r_sem, where):
@@ -110,6 +110,7 @@
     for sb, sx in peers:
         bb, xx = shifted(sb, sx)
         remote(own, own, gs_root, gr_root, dev(bb, xx, c)).start()
+    loaded(1, sliceb.at[x, c])
     own = sliceb.at[x, c]
     for sx in range(1, nx):
         bb, xx = shifted(0, sx)
@@ -169,22 +170,30 @@
         span = slice(first, first + count)
         k12, k13, v12 = ks.at[span, : 2 * D], ks.at[span, 2 * D :], vs.at[span, :]
 
-        def body(p):
-            rows = pl.ds(pl.multiple_of(p * pair, pair), pair)
+        def rows_of(p):
+            return pl.ds(pl.multiple_of(p * pair, pair), pair)
+
+        def key_side(p):
+            rows = rows_of(p)
             s = mm(k12[...], qt[0, :, rows]) + (mm(k12[...], qt[1, :, rows]) + mm(k13[...], qt[2, :, rows]))
             s = jnp.where(seen(count), s * scale, hidden)
             m = jnp.max(s, axis=0, keepdims=True)
-            g = mm(v12[...], ct[0, :, rows]) + mm(v12[...], ct[1, :, rows])
             e = jnp.exp(s - m)
             sc[span, rows] = e
-            dp[span, rows] = g
             top_c[chunk : chunk + 1, rows] = m
             sum_c[chunk : chunk + 1, rows] = jnp.sum(e, axis=0, keepdims=True)
-            dot_c[chunk : chunk + 1, rows] = jnp.sum(e * g, axis=0, keepdims=True)
+
+        def value_side(p):
+            rows = rows_of(p)
+            g = mm(v12[...], ct[0, :, rows]) + mm(v12[...], ct[1, :, rows])
+            dp[span, rows] = g
+            dot_c[chunk : chunk + 1, rows] = jnp.sum(sc[span, rows] * g, axis=0, keepdims=True)
 
         def trip(i, carry):
             for k in range(wide):
-                body(i * wide + k)
+                key_side(i * wide + k)
+            for k in range(wide):
+                value_side(i * wide + k)
             return carry
 
         if n_pair == wide:
@@ -268,20 +277,30 @@
     for i in range(1 + nx, len(chunks)):
         block_gradients(i)
     ex = []
-    if nc == 2:
-        ex.append(remote(root_g.at[:, :, other], rc_root, es_sem.at[0], er_sem.at[0], dev(b, x, other)))
-        ex[0].start()
+
+    def exchange(source, target):
+        if nc == 2:
+            i = len(ex)
+            ex.append(remote(source, target, es_sem.at[i], er_sem.at[i], dev(b, x, other)))
+            ex[i].start()
+
+    for k, sx in enumerate(columns):
+        bb, xx = shifted(0, sx)
+        exchange(root_g.at[:, xx, other], rc_root.at[k])
     for sx in range(nx):
         block_gradients(1 + sx)
-    if nc == 2:
-        ex.append(remote(slice_g.at[:, other], rc_slice, es_sem.at[1], er_sem.at[1], dev(b, x, other)))
-        ex[1].start()
-        ex[0].wait_recv()
-    mine = root_g[:, :, c]
-    sn_root[...] = mine + rc_root[...] if nc == 2 else mine
-    for i, (sb, sx) in enumerate(peers):
-        bb, xx = shifted(sb, sx)
-        remote(sn_root.at[bb, xx], rv_root.at[i], ss_root, sr_root, dev(bb, xx, c)).start()
+    exchange(slice_g.at[:, other], rc_slice)
+    for k, sx in enumerate(columns):
+        bb, xx = shifted(0, sx)
+        mine = root_g[:, xx, c]
+        if nc == 2:
+            ex[k].wait_recv()
+            mine = mine + rc_root[k]
+        sn_root[k] = mine
+        for i, (sb, sy) in enumerate(peers):
+            if sy == sx:
+                bb, xx = shifted(sb, sx)
+                remote(sn_root.at[k, bb], rv_root.at[i], ss_root, sr_root, dev(bb, xx, c)).start()
 
     stage_across(0, rootb[:, :, :, 0].reshape(n_root, D), rootb[:, :, :, 1].reshape(n_root, D))
     for sx in range(nx):
@@ -291,7 +310,7 @@
     stage_across(at_leaf, leaf_ref[0], leaf_ref[1])
 
     if nc == 2:
-        ex[1].wait_recv()
+        ex[nx].wait_recv()
     mine = slice_g[:, c]
     sn_slice[...] = mine + rc_slice[...] if nc == 2 else mine
     for sx in range(1, nx):
@@ -326,7 +345,7 @@
         for i in range(nx - 1):
             total = total + rv_slice[i]
     dslice_ref[...] = total
-    total = sn_root[b, x]
+    total = sn_root[nx - 1, b]
     if peers:
         remote(rv_root, rv_root, ss_root, sr_root, dev(b, x, c)).wait_recv()
         for i in range(len(peers)):
@@ -380,11 +399,11 @@
         V((n_keys, R), f32), V((n_keys, R), f32), V((n_root + n_slice, 2 * D), f32),
         V((n_chunks, R), f32), V((n_chunks, R), f32), V((n_chunks, R), f32), V((n_chunks, R), f32), V((1, R), f32),
         S((1,), jnp.int32), S((1,), jnp.int32), S((1,), jnp.int32),
-        V((nb, nx, r_rows, 2 * D), f32), V((nx, b_rows, 2 * D), f32),
-        V((nb, nx, r_rows, 2 * D), f32), V((nx, b_rows, 2 * D), f32),
+        V((nx, nb, r_rows, 2 * D), f32), V((nx, b_rows, 2 * D), f32),
+        V((nx, nb, r_rows, 2 * D), f32), V((nx, b_rows, 2 * D), f32),
         V((np_, r_rows, 2 * D), f32), V((max(nx - 1, 1), b_rows, 2 * D), f32),
         dma((7,)), dma, dma, dma, dma((nx,)), dma((1 + nx,)), dma((1 + nx,)),
-        dma, dma, dma, dma, dma((2,)), dma((2,)),
+        dma, dma, dma, dma, dma((1 + nx,)), dma((1 + nx,)),
     ]
     shape = lambda *s: V(s, f32)
     sizes = ((T, width), (T, width), (r_rows, 2 * D), (b_rows, 2 * D), (T, 2 * D))

time: 23.7 us -> 23.6 us (level)
  no operation moved by 1% of the time
where the time goes in v3:
time: 23.6 us; the launch traced here: 23.4 us
  Pallas kernels  20.8 us (88%)
  between operations  2.58 us (11%)
    pallas_call x1, Pallas kernels, shards(): pl.pallas_call(functools.partial(kernel, nb, nx, nc, (T, H, D, r_rows, b_...  19.7 us
    pallas_call x1, Pallas kernels, shards(): pl.pallas_call(deliver, out_shape=tuple((jax.ShapeDtypeStruct(size, f32)...  1.07 us

profile of v3, /device:TPU:0, one launch (start us, length us, event | category | flops | bytes accessed | tf_op | source)
XLA Modules:
  0.0 23.4 jit_solution(12645472278905839101)
XLA Ops:
  2.6 19.7 %tree.1 = (f32[128,1024]{1,0:T(8,128)S(1)}, f32[128,1024]{1,0:T(8,128)S(1)}, f32[16,256]{1,0:T(8,128)S(1)}, f32[64,256]{1,0:T(8,128)S(1)}, f32[128,256]{1,0:T(8,128)S(1)}) custom-call(f32[128,1024]{1,0:T(8,128)} %q_hbm.1, f32[128,128]{1,0:T(8,128)} %lk_hbm.1, f32[128,128]{1,0:T(8,128)} %lv_hbm.1, f32[16,128]{1,0:T(8,128)} %rk_hbm.1, f32[16,128]{1,0:T(8,128)} %rv_hbm.1, ...), custom_call_target="tpu_custom_call" | custom-call | tf_op jit(solution)/shard_map/tree/pallas_call | solution.py:410
  22.3 1.1 %deliver.1 = (f32[128,1024]{1,0:T(8,128)}, f32[128,1024]{1,0:T(8,128)}, f32[16,256]{1,0:T(8,128)}, f32[64,256]{1,0:T(8,128)}, f32[128,256]{1,0:T(8,128)}) custom-call(f32[128,1024]{1,0:T(8,128)S(1)} %get-tuple-element.10.refs_0_, f32[128,1024]{1,0:T(8,128)S(1)} %get-tuple-element.11.refs_1_, f32[16,256]{1,0:T(8,128)S(1)} %get-tuple-element.12.refs_2_, ...), custom_call_target="tpu_custom_call" | custom-call | tf_op jit(solution)/shard_map/deliver/pallas_call | solution.py:421
